TPU v7x, 32 devices: a whole 2x2x4 slice. The times are simulated.
32 devices in a mesh: grp: 4 (over z), dev: 8 (over y, x, core).
Axes of the slice: x: 2, y: 2, z: 4, core: 2. Of those that a mesh axis runs over, the one named last changes fastest.
Arguments:
- qkv_weight: bfloat16 [2, 4608, 8192], P(None, ('grp', 'dev')), may hold values from -0.09375 to 0.09375
- gate_up_weight: bfloat16 [2, 4608, 73728], P(None, ('grp', 'dev')), may hold values from -0.09375 to 0.09375
- head_slot: int32 [64], replicated, may hold values from 0 to 63, each once
- layer_ids: int32 [2], replicated, may hold values from 0 to 45
- stored_qkv: int32 [46, 64], replicated, may hold values from -16384 to 16383
- stored_gate_up: int32 [46, 576], replicated, may hold values from -16384 to 16383
Outputs:
- served_qkv: bfloat16 [2, 4608, 8192], P(None, 'grp', 'dev')
- served_gate_up: bfloat16 [2, 4608, 73728], P(None, 'grp', 'dev')
- qkv_mismatch: float32 [2, 64], P(None, 'dev')
- gate_up_mismatch: float32 [2, 576], P(None, 'dev')
Inputs may be any that keep to these rules, and one draw needn't show every extreme that they name: `head_slot`: each of the 64 heads appears once.
All inputs are finite; a program needn't handle non-finite values.
Results may differ from a plain program's by a relative error of at most 0.0004.
Values may be sent and summed in bfloat16 or wider, within the bound.
A program may use at most 256 MiB of HBM per device.

v0:
```python
import jax
import jax.numpy as jnp
from jax import lax
from jax.sharding import PartitionSpec as P

HEAD_DIM = 128
FF = 36864
STORED = 46
BLK = 128
NHEAD = 64
stored_unit = 1.0 / 1024.0


def finish(pieces):
    qkv_piece, gate_piece = pieces
    count = qkv_piece.shape[0]
    height = qkv_piece.shape[1]
    served_qkv = qkv_piece.reshape(count, height, qkv_piece.shape[4])
    served_gate = gate_piece.reshape(count, height, 2 * gate_piece.shape[4])
    return (served_qkv, served_gate)


def body(qkv_weight, gate_up_weight, head_slot, layer_ids, stored_qkv, stored_gate_up):
    owners = lax.axis_size("dev")
    owner = lax.axis_index("dev")
    layers = qkv_weight.shape[0]
    rows = qkv_weight.shape[1]
    slots = NHEAD // owners
    width = FF // owners
    blocks = width // BLK
    ordered = qkv_weight.reshape(layers, rows, NHEAD, HEAD_DIM)[:, :, head_slot, :]
    qkv_split = ordered.reshape(layers, rows, 1, owners, slots * HEAD_DIM)
    gate_split = gate_up_weight.reshape(layers, rows, 2, owners, width)
    moved = (
        lax.all_to_all(qkv_split, "dev", split_axis=3, concat_axis=1, tiled=True),
        lax.all_to_all(gate_split, "dev", split_axis=3, concat_axis=1, tiled=True),
    )
    results = finish(moved)
    served_qkv = results[0]
    served_gate = results[1]
    head_part = jnp.sum(ordered.astype(jnp.float32), axis=(1, 3))
    block_part = jnp.sum(
        gate_split.astype(jnp.float32).reshape(layers, rows, 2, owners, blocks, BLK), axis=(1, 5)
    )
    block_part = block_part.transpose(0, 2, 1, 3).reshape(layers, owners * 2 * blocks)
    head_all, block_all = lax.psum((head_part, block_part), ("grp", "dev"))
    head_sum = lax.dynamic_slice_in_dim(head_all, owner * slots, slots, 1)
    block_sum = lax.dynamic_slice_in_dim(block_all, owner * 2 * blocks, 2 * blocks, 1)
    layer_pick = (layer_ids[:, None] == jnp.arange(STORED, dtype=jnp.int32)[None, :]).astype(
        jnp.float32
    )
    picked_qkv = jnp.dot(
        layer_pick,
        stored_qkv.astype(jnp.float32),
        precision=lax.Precision.HIGHEST,
        preferred_element_type=jnp.float32,
    )
    picked_gate = jnp.dot(
        layer_pick,
        stored_gate_up.astype(jnp.float32),
        precision=lax.Precision.HIGHEST,
        preferred_element_type=jnp.float32,
    )
    own_heads = lax.dynamic_slice_in_dim(head_slot, owner * slots, slots, 0)
    picked_qkv = picked_qkv[:, own_heads]
    picked_gate = (
        picked_gate.reshape(layers, 2, owners, blocks)
        .transpose(0, 2, 1, 3)
        .reshape(layers, owners * 2 * blocks)
    )
    picked_gate = lax.dynamic_slice_in_dim(picked_gate, owner * 2 * blocks, 2 * blocks, 1)
    qkv_mismatch = head_sum - picked_qkv * stored_unit
    gate_up_mismatch = block_sum - picked_gate * stored_unit
    return (served_qkv, served_gate, qkv_mismatch, gate_up_mismatch)


def solution(mesh):
    placed = (P(None, ("grp", "dev"), None), P(None, ("grp", "dev"), None), P(), P(), P(), P())
    return jax.shard_map(
        body,
        mesh=mesh,
        in_specs=placed,
        out_specs=(P(None, "grp", "dev"), P(None, "grp", "dev"), P(None, "dev"), P(None, "dev")),
        check_vma=False,
    )
```

profile of v0, /device:TPU:0, one launch (start us, length us, event | category | flops | bytes accessed | tf_op | source)
XLA Modules:
  0.0 738.6 jit_solution(3566983164668967660)
XLA Ops:
  0.6 0.7 compare_select_fusion.1
  1.3 5.3 copy_bitcast_fusion
  6.6 5.7 gather_fusion
  12.3 6.3 copy.34
  18.6 8.2 %reshape.39 = bf16[2,144,1,8,1024]{4,3,1,0,2:T(8,128)(2,1)} reshape(bf16[2,144,64,128]{3,2,1,0:T(8,128)(2,1)} %copy.34) | data formatting | bytes 9437184 | tf_op jit(solution)/shard_map/reshape | solution.py:32
  26.8 7.1 copy.35
  33.9 5.2 all-to-all-start
  39.1 29.1 %copy.45 = bf16[36,8,16,4608]{3,2,1,0:T(8,128)(2,1)} copy(bf16[36,8,16,4608]{3,1,2,0:T(8,128)(2,1)} %bitcast.27) | data formatting | bytes 84934656
  68.2 59.8 %copy.37 = bf16[2,144,2,8,4608]{4,2,1,0,3:T(2,128)(2,1)} copy(bf16[2,144,2,8,4608]{4,3,2,1,0:T(8,128)(2,1)} %bitcast.28) | data formatting | bytes 84934656 | tf_op jit(solution)/shard_map/reshape | solution.py:33
  128.0 0.0 copy-start
  128.0 0.0 copy-start.1
  128.0 0.0 all-to-all-done
  128.1 8.2 %all-to-all-start.1 = ((bf16[2,144,2,8,4608]{4,2,1,0,3:T(2,128)(2,1)}), bf16[2,144,2,8,4608]{4,2,1,0,3:T(2,128)(2,1)}, u32[]{:S(2)}, u32[]{:S(2)}) async-start(bf16[2,144,2,8,4608]{4,2,1,0,3:T(2,128)(2,1)} %copy.37), calls=%async_computation.1 | async-start | bytes 84934656 | tf_op jit(solution)/shard_map/all_to_all | solution.py:36
  136.2 0.0 copy-done
  136.2 0.0 copy-done.1
  136.2 0.2 fusion
  136.4 0.1 reshape.44
  136.6 0.1 reshape.45
  136.7 0.0 copy-start.3
  136.7 0.0 copy-start.2
  136.7 14.8 %convert_reduce_fusion = f32[2,73728]{1,0:T(2,128)S(1)} fusion(bf16[2,144,73728]{2,1,0:T(8,128)(2,1)} %param.7), kind=kLoop, calls=%fused_computation.2 | loop fusion | flops 42319872 | bytes 43057152 | tf_op jit(solution)/shard_map/reduce_sum | solution.py:42
  151.5 0.5 reduce_sum.27
  152.0 0.2 reduce_sum.28
  152.2 0.1 reshape.43
  152.3 0.0 copy-done.3
  152.4 0.1 compare_select_fusion
  152.4 0.0 copy-done.2
  152.4 0.2 fusion.2
  152.7 0.6 gather_fusion.1
  153.2 3.1 convert_reduce_fusion.1
  156.4 473.4 %all-reduce = (f32[2,64]{0,1:T(8,128)S(1)}, f32[2,576]{1,0:T(2,128)S(1)}) all-reduce(f32[2,64]{0,1:T(8,128)S(1)} %convert_reduce_fusion.1, f32[2,576]{1,0:T(2,128)S(1)} %reshape.43), channel_id=1, replica_groups=mesh['grp'=4,'dev'=8] {'grp','dev'}, use_global_device_ids=true, to_apply=%region_1.0 | all-reduce | flops 1280 | bytes 10240 | tf_op jit(solution)/shard_map/psum | solution.py:46
  629.8 0.6 copy.42
  630.4 0.6 multiply_subtract_fusion
  631.1 5.2 copy.36
  636.3 0.0 all-to-all-done.1
  636.3 36.7 %copy.38 = bf16[2,8,144,2,1,4608]{5,3,2,1,0,4:T(2,128)(2,1)} copy(bf16[2,8,144,2,1,4608]{5,3,2,0,1,4:T(2,128)(2,1)} %bitcast.5) | data formatting | bytes 84934656 | tf_op jit(solution)/shard_map/all_to_all | solution.py:36
  673.0 65.6 %reshape.42 = bf16[2,1152,9216]{2,1,0:T(8,128)(2,1)} reshape(bf16[2,8,144,2,1,4608]{5,3,2,1,0,4:T(2,128)(2,1)} %copy.38) | data formatting | bytes 84934656 | tf_op jit(solution)/shard_map/reshape | solution.py:19
  (5 shorter events, 0.0 us)
Async XLA Ops:
  33.9 94.1 %all-to-all-start = ((bf16[2,144,1,8,1024]{4,1,0,2,3:T(8,128)(2,1)}), bf16[2,144,1,8,1024]{4,1,0,2,3:T(8,128)(2,1)}, u32[]{:S(2)}, u32[]{:S(2)}) async-start(bf16[2,144,1,8,1024]{4,1,0,2,3:T(8,128)(2,1)} %copy.35), calls=%async_computation | async-start | bytes 9437184 | tf_op jit(solution)/shard_map/all_to_all | solution.py:35
  128.0 8.2 %copy-start = (s32[46,576]{1,0:T(8,128)S(1)}, s32[46,576]{1,0:T(8,128)}, u32[]{:S(2)}) copy-start(s32[46,576]{1,0:T(8,128)} %param.11) | copy-start | bytes 317956
  128.0 8.2 %copy-start.1 = (s32[2]{0:T(128)S(1)}, s32[2]{0:T(128)}, u32[]{:S(2)}) copy-start(s32[2]{0:T(128)} %param.9) | copy-start | bytes 28
  128.1 508.3 %all-to-all-start.1 = ((bf16[2,144,2,8,4608]{4,2,1,0,3:T(2,128)(2,1)}), bf16[2,144,2,8,4608]{4,2,1,0,3:T(2,128)(2,1)}, u32[]{:S(2)}, u32[]{:S(2)}) async-start(bf16[2,144,2,8,4608]{4,2,1,0,3:T(2,128)(2,1)} %copy.37), calls=%async_computation.1 | async-start | bytes 84934656 | tf_op jit(solution)/shard_map/all_to_all | solution.py:36
  136.7 15.7 %copy-start.3 = (s32[64]{0:T(128)S(1)}, s32[64]{0:T(128)}, u32[]{:S(2)}) copy-start(s32[64]{0:T(128)} %param.8) | copy-start | bytes 772
  136.7 15.8 %copy-start.2 = (s32[46,64]{1,0:T(8,128)S(1)}, s32[46,64]{1,0:T(8,128)}, u32[]{:S(2)}) copy-start(s32[46,64]{1,0:T(8,128)} %param.10) | copy-start | bytes 35332
where the time goes:
time: 741 us; the launch traced here: 739 us
  blocking collectives  473 us (64%)
  local copies, waits for them, and re-layouts  231 us (31%)
  other arithmetic  19.6 us (3%)
  starting transfers between devices  13.4 us (2%)
    psum x1, blocking collectives, body(): head_all, block_all = lax.psum((head_part, block_part), ('grp', 'dev'))  473 us
    reshape x1, local copies, waits for them, and re-layouts, finish(): served_gate = gate_piece.reshape(count, height, 2 * gate_piece.shape[4])  65.6 us
    reshape x1, local copies, waits for them, and re-layouts, body(): gate_split = gate_up_weight.reshape(layers, rows, 2, owners, width)  59.8 us
    all_to_all x1, local copies, waits for them, and re-layouts, body(): lax.all_to_all(gate_split, 'dev', split_axis=3, concat_axis=1, tiled=True)  36.7 us
    unnamed x10, local copies, waits for them, and re-layouts  29.7 us
    reshape x2, local copies, waits for them, and re-layouts, body(): qkv_split = ordered.reshape(layers, rows, 1, owners, slots * HEAD_DIM)  15.3 us
    reduce_sum x2, other arithmetic, body(): jnp.sum(gate_split.astype(jnp.float32).reshape(layers, rows, 2, owners, b...  15 us
  transfers between devices with their start and end apart: 2, of which 0 were waited for; matrix products, arithmetic and copies ran while one was open for 16% of the time, Pallas kernels for 0%

commit v1 on v0

--- a/solution.py
+++ b/solution.py
@@ -33,7 +33,12 @@
     gate_split = gate_up_weight.reshape(layers, rows, 2, owners, width)
     moved = (
         lax.all_to_all(qkv_split, "dev", split_axis=3, concat_axis=1, tiled=True),
-        lax.all_to_all(gate_split, "dev", split_axis=3, concat_axis=1, tiled=True),
+        jnp.concatenate(
+            lax.all_to_all(
+                jnp.stack(jnp.split(gate_split, lax.axis_size("dev"), axis=3)), "dev", 0, 0
+            ),
+            axis=1,
+        ),
     )
     results = finish(moved)
     served_qkv = results[0]

time: 741 us -> 955 us (1.29)
  local copies, waits for them, and re-layouts: 231 us -> 444 us
    another operation x0 -> x3, local copies, waits for them, and re-layouts: none -> 146 us  [the longest x2 80.4 us: body(): jnp.stack(jnp.split(gate_split, lax.axis_size('dev'), axis=3))]
    split x0 -> x1, local copies, waits for them, and re-layouts: none -> 137 us  [body(): jnp.split(gate_split, lax.axis_size('dev'), axis=3)]
    reshape x2 -> x1, local copies, waits for them, and re-layouts: 125 us -> 36.7 us  [body(): jnp.concatenate(lax.all_to_all(jnp.stack(jnp.split(gate_split, lax.axis_s...]
    unnamed x10 -> x17, local copies, waits for them, and re-layouts: 29.7 us -> 85.4 us
    all_to_all x1 -> x0, local copies, waits for them, and re-layouts: 36.7 us -> none  [body(): lax.all_to_all(gate_split, 'dev', split_axis=3, concat_axis=1, tiled=True)]
  transfers between devices with their start and end apart: 2 -> 2, of which waited for: 0 -> 0; matrix products, arithmetic and copies ran while one was open for 16% -> 35% of each run, Pallas kernels for 0% -> 0%
where the time goes in v1:
time: 955 us; the launch traced here: 952 us
  blocking collectives  474 us (50%)
  local copies, waits for them, and re-layouts  444 us (46%)
  other arithmetic  19.6 us (2%)
  starting transfers between devices  13 us (1%)
    psum x1, blocking collectives, body(): head_all, block_all = lax.psum((head_part, block_part), ('grp', 'dev'))  474 us
    split x1, local copies, waits for them, and re-layouts, body(): jnp.split(gate_split, lax.axis_size('dev'), axis=3)  137 us
    unnamed x17, local copies, waits for them, and re-layouts  85.4 us
    another operation x2, local copies, waits for them, and re-layouts, body(): jnp.stack(jnp.split(gate_split, lax.axis_size('dev'), axis=3))  80.4 us
    another operation x1, local copies, waits for them, and re-layouts, finish(): served_gate = gate_piece.reshape(count, height, 2 * gate_piece.shape[4])  65.6 us
    reshape x1, local copies, waits for them, and re-layouts, body(): jnp.concatenate(lax.all_to_all(jnp.stack(jnp.split(gate_split, lax.axis_s...  36.7 us
  transfers between devices with their start and end apart: 2, of which 0 were waited for; matrix products, arithmetic and copies ran while one was open for 35% of the time, Pallas kernels for 0%

profile of v1, /device:TPU:0, one launch (start us, length us, event | category | flops | bytes accessed | tf_op | source)
XLA Modules:
  0.0 951.9 jit_solution(13559149965136919080)
XLA Ops:
  0.6 5.3 copy_bitcast_fusion
  6.0 0.7 compare_select_fusion.1
  6.6 5.7 gather_fusion
  12.3 6.3 copy.211
  18.6 8.2 reshape.38
  26.8 7.1 copy.212
  33.9 5.2 all-to-all-start
  39.1 29.1 %copy.230 = bf16[36,8,16,4608]{3,2,1,0:T(8,128)(2,1)} copy(bf16[36,8,16,4608]{3,1,2,0:T(8,128)(2,1)} %bitcast.42) | data formatting | bytes 84934656
  68.2 136.7 %fusion.6 = (bf16[2,144,2,1,4608]{4,3,2,1,0:T(2,128)(2,1)S(1)}, bf16[2,144,2,1,4608]{4,3,2,1,0:T(2,128)(2,1)}, bf16[2,144,2,1,4608]{4,3,2,1,0:T(2,128)(2,1)}, bf...) fusion(bf16[2,144,2,8,4608]{4,3,2,1,0:T(8,128)(2,1)} %bitcast.41), kind=kLoop, calls=%fused_computation.26 | loop fusion | bytes 84934656 | tf_op jit(solution)/shard_map/split | solution.py:38
  205.0 8.0 bitcast_dynamic-update-slice_fusion.7
  212.9 8.0 bitcast_dynamic-update-slice_fusion.6
  220.9 8.0 bitcast_dynamic-update-slice_fusion.5
  228.8 8.0 bitcast_dynamic-update-slice_fusion.4
  236.8 8.0 bitcast_dynamic-update-slice_fusion.3
  244.7 8.0 bitcast_dynamic-update-slice_fusion.2
  252.7 8.0 bitcast_dynamic-update-slice_fusion.1
  260.6 4.2 bitcast_dynamic-update-slice_fusion
  264.8 76.2 %copy.222 = bf16[8,2,144,2,1,4608]{5,3,2,1,4,0:T(2,128)(2,1)} copy(bf16[8,2,144,2,1,4608]{5,2,4,3,1,0:T(8,128)(2,1)} %bitcast_dynamic-update-slice_fusion) | data formatting | bytes 84934656 | tf_op jit(solution)/shard_map/stack | solution.py:38
  341.0 0.0 all-to-all-done
  341.0 7.8 all-to-all-start.1
  348.9 0.0 copy-start.3
  348.9 0.0 copy-start.1
  348.9 0.0 copy-start.2
  348.9 0.0 copy-start
  348.9 14.8 %convert_reduce_fusion = f32[2,73728]{1,0:T(2,128)S(1)} fusion(bf16[2,144,73728]{2,1,0:T(8,128)(2,1)} %param.7), kind=kLoop, calls=%fused_computation.2 | loop fusion | flops 42319872 | bytes 43057152 | tf_op jit(solution)/shard_map/reduce_sum | solution.py:47
  363.7 0.5 reduce_sum.27
  364.2 0.2 reduce_sum.28
  364.5 0.1 reshape.42
  364.6 0.0 copy-done.3
  364.6 0.1 compare_select_fusion
  364.7 0.0 copy-done.1
  364.7 0.0 copy-done.2
  364.7 0.2 fusion.2
  364.9 0.6 gather_fusion.1
  365.5 3.1 convert_reduce_fusion.1
  368.6 474.0 %all-reduce = (f32[2,64]{0,1:T(8,128)S(1)}, f32[2,576]{1,0:T(2,128)S(1)}) all-reduce(f32[2,64]{0,1:T(8,128)S(1)} %convert_reduce_fusion.1, f32[2,576]{1,0:T(2,128)S(1)} %reshape.42), channel_id=1, replica_groups=mesh['grp'=4,'dev'=8] {'grp','dev'}, use_global_device_ids=true, to_apply=%region_1.0 | all-reduce | flops 1280 | bytes 10240 | tf_op jit(solution)/shard_map/psum | solution.py:51
  842.6 0.6 copy.227
  843.3 0.0 copy-done
  843.3 0.2 fusion
  843.5 0.1 reshape.43
  843.6 0.1 reshape.44
  843.7 0.6 multiply_subtract_fusion
  844.3 5.2 copy.213
  849.6 0.0 all-to-all-done.1
  849.6 36.7 %copy.223 = bf16[2,8,144,2,1,4608]{5,3,2,1,0,4:T(2,128)(2,1)} copy(bf16[2,8,144,2,1,4608]{5,3,2,0,4,1:T(2,128)(2,1)} %bitcast.12) | data formatting | bytes 84934656 | tf_op jit(solution)/shard_map/reshape | solution.py:36
  886.3 65.6 %reshape_reshape.3 = bf16[2,1152,9216]{2,1,0:T(8,128)(2,1)} reshape(bf16[2,8,144,2,1,4608]{5,3,2,1,0,4:T(2,128)(2,1)} %copy.223) | data formatting | bytes 84934656 | tf_op jit(solution)/shard_map/reshape;reshape | solution.py:19
  (5 shorter events, 0.0 us)
Async XLA Ops:
  33.9 307.1 %all-to-all-start = ((bf16[2,144,1,8,1024]{4,1,0,2,3:T(8,128)(2,1)}), bf16[2,144,1,8,1024]{4,1,0,2,3:T(8,128)(2,1)}, u32[]{:S(2)}, u32[]{:S(2)}) async-start(bf16[2,144,1,8,1024]{4,1,0,2,3:T(8,128)(2,1)} %copy.212), calls=%async_computation | async-start | bytes 9437184 | tf_op jit(solution)/shard_map/all_to_all | solution.py:35
  341.0 508.5 %all-to-all-start.1 = ((bf16[8,2,144,2,1,4608]{5,3,2,1,4,0:T(2,128)(2,1)}), bf16[8,2,144,2,1,4608]{5,3,2,1,4,0:T(2,128)(2,1)}, u32[]{:S(2)}, u32[]{:S(2)}) async-start(bf16[8,2,144,2,1,4608]{5,3,2,1,4,0:T(2,128)(2,1)} %copy.222), calls=%async_computation.1 | async-start | bytes 84934656 | tf_op jit(solution)/shard_map/all_to_all | solution.py:37
  348.9 15.7 %copy-start.3 = (s32[64]{0:T(128)S(1)}, s32[64]{0:T(128)}, u32[]{:S(2)}) copy-start(s32[64]{0:T(128)} %param.8) | copy-start | bytes 772
  348.9 15.8 %copy-start.1 = (s32[2]{0:T(128)S(1)}, s32[2]{0:T(128)}, u32[]{:S(2)}) copy-start(s32[2]{0:T(128)} %param.9) | copy-start | bytes 28
  348.9 15.8 %copy-start.2 = (s32[46,64]{1,0:T(8,128)S(1)}, s32[46,64]{1,0:T(8,128)}, u32[]{:S(2)}) copy-start(s32[46,64]{1,0:T(8,128)} %param.10) | copy-start | bytes 35332
  348.9 494.3 %copy-start = (s32[46,576]{1,0:T(8,128)S(1)}, s32[46,576]{1,0:T(8,128)}, u32[]{:S(2)}) copy-start(s32[46,576]{1,0:T(8,128)} %param.11) | copy-start | bytes 317956
